TPU v7x, 512 devices: a whole 4x4x16 slice. The times are simulated.
512 devices in a mesh: src: 8 (over x, core), tgt: 64 (over y, z).
Axes of the slice: x: 4, y: 4, z: 16, core: 2. Of those that a mesh axis runs over, the one named last changes fastest.
Arguments:
- source_points: float32 [32, 16384], P(None, ('src', 'tgt')), may hold values from -1.25 to 1.25
- target_points: float32 [32, 65536], P('src', 'tgt'), may hold values from -1.2 to 1.2
- source_potential: float32 [16384], P(('src', 'tgt')), may hold values from -1.5 to 1.5
- target_potential: float32 [65536], P('tgt'), may hold values from -1.5 to 1.5
- source_weight: float32 [16384], P(('src', 'tgt')), may hold values from 0.5 to 2
- target_weight: float32 [65536], P('tgt'), may hold values from 0.5 to 2
- core_previous: float32 [34, 34], replicated, may hold values from -0.12 to 0.12
Outputs:
- source_new: float32 [16384], P(('src', 'tgt'))
- target_new: float32 [65536], P('tgt')
- core_new: float32 [34, 34], replicated
All inputs are finite; a program needn't handle non-finite values.
Results may differ from a plain program's by a relative error of at most 0.0002.
Values sent between devices are 32-bit elements; how exact they have to be, the bound alone decides.
No kernel may reach another device: no remote copies, remote signals or barrier semaphores. Data moves between devices by JAX's collectives and lax.ppermute only.
A program may use at most 64 MiB of HBM per device.

v0:
```python
import functools
import jax
import jax.numpy as jnp
from jax import lax
from jax.sharding import Mesh
from jax.sharding import PartitionSpec as P

TGT = ("tgt_0", "tgt_1")
SRC = ("src_0", "src_1")
SRC_TGT = ("src_0", "src_1", "tgt_0", "tgt_1")
EPSILON = 0.5
HIGHEST = lax.Precision.HIGHEST


def rows_first(arrays, axis, dims):
    turned = [jnp.moveaxis(a, dim, 0) for a, dim in zip(arrays, dims)]
    both = jnp.concatenate([t.reshape(len(t), -1) for t in turned], axis=1)
    filled, at, gathered = (lax.all_gather(both, axis, axis=0, tiled=True), 0, [])
    for t, dim in zip(turned, dims):
        slab = filled[:, at : at + t[0].size].reshape(-1, *t.shape[1:])
        gathered.append(jnp.moveaxis(slab, 0, dim))
        at += t[0].size
    return tuple(gathered)


def sent_to_all(x, axis):
    copies = jnp.broadcast_to(x, (lax.axis_size(axis), *x.shape))
    return lax.all_to_all(copies, axis, split_axis=0, concat_axis=0, tiled=True)


def laid_out(parts, dim):
    parts = jnp.moveaxis(parts, 0, dim)
    dims = parts.shape
    return parts.reshape(*dims[:dim], dims[dim] * dims[dim + 1], *dims[dim + 2 :])


def collect(x, axis, dim):
    parts = sent_to_all(x, axis)
    return laid_out(parts, dim)


def by_axis(x, axes):
    return functools.reduce(lax.psum, axes, x)


def collected_together(x, axis):
    leaves = jax.tree.leaves(x)
    sequence = sorted(range(len(leaves)), key=lambda k: -leaves[k].size)
    width = (1, *leaves[sequence[0]].shape)[-1]
    lines = [
        jnp.pad(leaves[k].reshape(-1), (0, -leaves[k].size % width)).reshape(-1, width)
        for k in sequence
    ]
    both, at, found = (lax.all_gather(jnp.concatenate(lines), axis), 0, {})
    for k, line in zip(sequence, lines):
        slab = both[:, at : at + len(line)].reshape(len(both), -1)
        found[k] = slab[:, : leaves[k].size].reshape(-1, *leaves[k].shape)
        at += len(line)
    numbers = iter(range(len(leaves)))
    return jax.tree.map(lambda _: found[next(numbers)], x)


def joined_all(x, axes, combine):
    for axis in axes:
        pieces = collected_together(x, axis)
        x = jax.tree.map(lambda part: part[0], pieces)
        for k in range(1, lax.axis_size(axis)):
            x = combine(x, jax.tree.map(lambda part: part[k], pieces))
    return x


def all_in_one(x, axis):
    leaves = jax.tree.leaves(x)
    sequence = sorted(range(len(leaves)), key=lambda k: -leaves[k].size)
    width = (1, *leaves[sequence[0]].shape)[-1]
    lines = [
        jnp.pad(leaves[k].reshape(-1), (0, -leaves[k].size % width)).reshape(-1, width)
        for k in sequence
    ]
    both, at, found = (sent_to_all(jnp.concatenate(lines), axis), 0, {})
    for k, line in zip(sequence, lines):
        slab = both[:, at : at + len(line)].reshape(len(both), -1)
        found[k] = slab[:, : leaves[k].size].reshape(-1, *leaves[k].shape)
        at += len(line)
    numbers = iter(range(len(leaves)))
    return jax.tree.map(lambda _: found[next(numbers)], x)


def combined_pairwise(pieces, combine):
    while len(jax.tree.leaves(pieces)[0]) > 1:
        pieces = jax.vmap(combine)(
            *(jax.tree.map(lambda part: part[side::2], pieces) for side in (0, 1))
        )
    return jax.tree.map(lambda part: part[0], pieces)


def combined_all(x, axis, combine):
    pieces = all_in_one(x, axis)
    return combined_pairwise(pieces, combine)


def factors(points):
    squares = jnp.sum(points * points, axis=0, keepdims=True)
    unit_row = jnp.ones_like(squares)
    return (
        jnp.concatenate([squares, unit_row, -2.0 * points], 0),
        jnp.concatenate([unit_row, squares, points], 0),
    )


def contract_rank(left_block, weighted):
    return lax.dot_general(
        left_block,
        weighted,
        (((0,), (0,)), ((), ())),
        precision=HIGHEST,
        preferred_element_type=jnp.float32,
    )


def contract_last(former, latter):
    return lax.dot_general(
        former,
        latter,
        (((1,), (1,)), ((), ())),
        precision=HIGHEST,
        preferred_element_type=jnp.float32,
    )


def row_blocks(values, block_size):
    number = values.shape[-1] // block_size
    shaped = values.reshape(values.shape[:-1] + (number, block_size))
    return jnp.moveaxis(shaped, -2, 0)


def combine_parts(former, latter):
    highest = jnp.maximum(former[0], latter[0])
    return (
        highest,
        former[1] * jnp.exp(former[0] - highest) + latter[1] * jnp.exp(latter[0] - highest),
    )


def on_device(
    source_points,
    target_points,
    source_potential,
    target_potential,
    source_weight,
    target_weight,
    core_previous,
):
    spread = lax.axis_size(TGT)
    sources = source_points.shape[1] * spread * lax.axis_size(SRC)
    targets = target_potential.shape[0] * spread
    points, potential, weight = rows_first(
        (source_points, source_potential, source_weight), TGT, (1, 0, 0)
    )
    features = collect(target_points, SRC, 0)
    log_source = jnp.log(weight) - jnp.log(jnp.float32(sources))
    log_target = jnp.log(target_weight) - jnp.log(jnp.float32(targets))
    left_source, right_source = factors(points)
    left_target, right_target = factors(features)
    row_count = points.shape[1]
    share_count = row_count // spread
    block_size = min(512, row_count)
    left_blocks = row_blocks(left_source, block_size)
    right_blocks = row_blocks(right_source, block_size)
    potential_blocks = row_blocks(potential, block_size)
    weight_blocks = row_blocks(log_source, block_size)
    rank_size = left_source.shape[0]
    previous_w = jnp.dot(core_previous, left_target, precision=HIGHEST)

    def plan_step(running, portion):
        left_block, right_block, source_part, log_weight = portion
        scores = contract_rank(left_block, previous_w)
        plan_tile = jnp.exp(
            log_weight[:, None]
            + log_target[None, :]
            + (source_part[:, None] + target_potential[None, :] + 2.0 * scores) / EPSILON
        )
        carried = contract_last(right_target, plan_tile)
        return (running + contract_last(right_block, carried), None)

    partial_core, _ = lax.scan(
        plan_step,
        jnp.zeros((rank_size, rank_size), jnp.float32),
        (left_blocks, right_blocks, potential_blocks, weight_blocks),
    )
    core_new = by_axis(partial_core, SRC_TGT)
    current = jnp.dot(core_new, left_target, precision=HIGHEST)

    def row_step(left_block):
        scores = (
            log_target[None, :]
            + (target_potential[None, :] + 2.0 * contract_rank(left_block, current)) / EPSILON
        )
        maxima = jnp.max(scores, axis=1)
        return (maxima, jnp.sum(jnp.exp(scores - maxima[:, None]), axis=1))

    local_max, local_sum = lax.map(row_step, left_blocks)
    local_max = local_max.reshape(row_count)
    local_sum = local_sum.reshape(row_count)
    offset = lax.axis_index(TGT) * share_count
    highest, summed = joined_all((local_max, local_sum), TGT, combine_parts)
    source_new = EPSILON * (log_source - highest - jnp.log(summed))
    own_rows = lax.dynamic_slice_in_dim(source_new, offset, share_count)
    new_blocks = row_blocks(source_new, block_size)

    def column_step(state, portion):
        maxima, totals = state
        left_block, log_weight, source_part = portion
        scores = (
            log_weight[:, None]
            + (source_part[:, None] + 2.0 * contract_rank(left_block, current)) / EPSILON
        )
        highest = jnp.maximum(maxima, jnp.max(scores, axis=0))
        totals = totals * jnp.exp(maxima - highest) + jnp.sum(
            jnp.exp(scores - highest[None, :]), axis=0
        )
        return ((highest, totals), None)

    columns = target_potential.shape[0]
    start = (jnp.full((columns,), -jnp.inf, jnp.float32), jnp.zeros((columns,), jnp.float32))
    (column_max, column_total), _ = lax.scan(
        column_step, start, (left_blocks, weight_blocks, new_blocks)
    )
    highest, summed = combined_all((column_max, column_total), SRC, combine_parts)
    target_new = EPSILON * (log_target - highest - jnp.log(summed))
    return (own_rows, target_new, core_new)


def solution(mesh):
    finer = Mesh(mesh.devices.reshape(4, 2, 4, 16), ("src_0", "src_1", "tgt_0", "tgt_1"))
    placed = (P(None, SRC_TGT), P(SRC, TGT), P(SRC_TGT), P(TGT), P(SRC_TGT), P(TGT), P())
    return jax.shard_map(
        on_device, mesh=finer, in_specs=placed, out_specs=(P(SRC_TGT), P(TGT), P()), check_vma=False
    )
```

profile of v0, /device:TPU:1, one launch (start us, length us, event | category | flops | bytes accessed | tf_op | source)
XLA Modules:
  0.0 303.7 jit_solution(410053554644530980)
XLA Ops:
  2.0 10.1 %all-to-all-start = ((f32[8,4,1024]{2,1,0:T(4,128)}), f32[8,4,1024]{2,1,0:T(4,128)S(1)}, u32[]{:S(2)}, u32[]{:S(2)}) async-start(f32[8,4,1024]{2,1,0:T(4,128)} %broadcast_in_dim.44), calls=%async_computation | async-start | bytes 262144 | tf_op jit(solution)/shard_map/all_to_all | solution.py:28
  14.5 77.8 %all_gather.15 = f32[2048,34]{1,0:T(8,128)S(1)} all-gather(f32[32,34]{1,0:T(8,128)S(1)} %pad_maximum_fusion.4), channel_id=1, replica_groups=mesh['src_0'=4,'src_1'=2,'tgt_0'=4,'tgt_1'=16] {'tgt_0','tgt_1'}, dimensions={0}, use_global_device_ids=true | all-gather | bytes 282880 | tf_op jit(solution)/shard_map/all_gather | solution.py:18
  95.0 19.5 %while.37 = (s32[]{:T(128)}, f32[34,34]{1,0:T(8,128)S(1)}, f32[4,34,512]{2,0,1:T(4,128)S(1)}, f32[4,512]{1,0:T(4,128)S(1)}, f32[1024]{0:T(1024)S(1)}, /*index=5*...) while((s32[]{:T(128)}, f32[34,34]{1,0:T(8,128)S(1)}, ...), condition=%wide.region_3.4_spmd.clone, body=%wide.region_2.3_spmd.clone.sunk | while | flops 438069504 | bytes 4957355 | solution.py:186
  96.9 2.7 fusion.111
  101.8 2.7 fusion.111
  106.7 2.7 fusion.111
  111.5 2.7 fusion.111
  114.5 13.5 %psum.28 = f32[34,34]{1,0:T(8,128)S(1)} all-reduce(f32[34,34]{1,0:T(8,128)S(1)} %get-tuple-element.131), channel_id=1, replica_groups=mesh['src_0'=4,'src_1'=2,'tgt_0'=4,'tgt_1'=16] {'src_0'}, use_global_device_ids=true, to_apply=%region_4.5 | all-reduce | flops 1156 | bytes 9248 | tf_op jit(solution)/shard_map/psum | solution.py:43
  128.0 32.6 %psum.29 = f32[34,34]{1,0:T(8,128)S(1)} all-reduce(f32[34,34]{1,0:T(8,128)S(1)} %psum.28), channel_id=1, replica_groups=mesh['src_0'=4,'src_1'=2,'tgt_0'=4,'tgt_1'=16] {'src_1'}, use_global_device_ids=true, to_apply=%region_5.6 | all-reduce | flops 1156 | bytes 9248 | tf_op jit(solution)/shard_map/psum | solution.py:43
  160.7 12.5 %psum.30 = f32[34,34]{1,0:T(8,128)S(1)} all-reduce(f32[34,34]{1,0:T(8,128)S(1)} %psum.29), channel_id=1, replica_groups=mesh['src_0'=4,'src_1'=2,'tgt_0'=4,'tgt_1'=16] {'tgt_0'}, use_global_device_ids=true, to_apply=%region_6.7 | all-reduce | flops 1156 | bytes 9248 | tf_op jit(solution)/shard_map/psum | solution.py:43
  173.2 39.7 %psum.31 = f32[34,34]{1,0:T(8,128)S(1)} all-reduce(f32[34,34]{1,0:T(8,128)S(1)} %psum.30), channel_id=1, replica_groups=mesh['src_0'=4,'src_1'=2,'tgt_0'=4,'tgt_1'=16] {'tgt_1'}, use_global_device_ids=true, to_apply=%region_7.8 | all-reduce | flops 1156 | bytes 9248 | tf_op jit(solution)/shard_map/psum | solution.py:43
  213.5 11.3 %while.36 = (s32[]{:T(128)}, f32[4,512]{1,0:T(4,128)S(1)}, f32[4,512]{1,0:T(4,128)S(1)}, f32[1024]{0:T(1024)S(1)}, f32[1024]{0:T(1024)S(1)}, /*index=5*/f32[4,34...) while((s32[]{:T(128)}, f32[4,512]{1,0:T(4,128)S(1)}, f32[4,512]{1,0:T(4,128)S(1)}, ...), condition=%wide.region_11.12_spmd, body=%wide.region_8.11_spmd.sunk | while | flops 217578496 | bytes 4462697 | solution.py:202
  213.5 2.2 fusion.104
  216.3 2.2 fusion.104
  219.1 2.2 fusion.104
  222.0 2.2 fusion.104
  224.9 9.0 %all-gather.2 = f32[4,2,2048]{2,1,0:T(2,128)S(1)} all-gather(f32[1,2,2048]{2,1,0:T(2,128)S(1)} %maximum_bitcast_fusion.2), channel_id=2, replica_groups=mesh['src_0'=4,'src_1'=2,'tgt_0'=4,'tgt_1'=16] {'tgt_0'}, dimensions={0}, use_global_device_ids=true | all-gather | bytes 81920 | tf_op jit(solution)/shard_map/all_gather | solution.py:54
  233.9 20.8 %all-gather.3 = f32[16,2,2048]{2,1,0:T(2,128)S(1)} all-gather(f32[1,2,2048]{2,1,0:T(2,128)S(1)} %maximum_bitcast_fusion.3), channel_id=3, replica_groups=mesh['src_0'=4,'src_1'=2,'tgt_0'=4,'tgt_1'=16] {'tgt_1'}, dimensions={0}, use_global_device_ids=true | all-gather | bytes 278528 | tf_op jit(solution)/shard_map/all_gather | solution.py:54
  256.2 10.2 %while.38 = (s32[]{:T(128)}, f32[1024]{0:T(1024)S(1)}, f32[1024]{0:T(1024)S(1)}, f32[4,512]{1,0:T(4,128)S(1)}, f32[4,512]{1,0:T(4,128)S(1)}, /*index=5*/f32[4,34...) while((s32[]{:T(128)}, f32[1024]{0:T(1024)S(1)}, f32[1024]{0:T(1024)S(1)}, ...), condition=%wide.region_15.16_spmd.clone, body=%wide.region_12.15_spmd.clone.sunk | while | flops 217584640 | bytes 4505712 | solution.py:226
  258.8 2.1 fusion.113
  261.4 2.1 fusion.113
  263.9 2.1 fusion.113
  267.1 30.7 %all-to-all-start.1 = ((f32[8,2,1024]{2,1,0:T(2,128)}), f32[8,2,1024]{2,1,0:T(2,128)S(1)}, u32[]{:S(2)}, u32[]{:S(2)}) async-start(f32[8,2,1024]{2,1,0:T(2,128)} %broadcast_in_dim.49), calls=%async_computation.1 | async-start | bytes 131072 | tf_op jit(solution)/shard_map/all_to_all | solution.py:28
  298.6 4.1 %all-to-all-done.1 = f32[8,2,1024]{2,1,0:T(2,128)S(1)} async-done(((f32[8,2,1024]{2,1,0:T(2,128)}), f32[8,2,1024]{2,1,0:T(2,128)S(1)}, u32[]{:S(2)}, u32[]{:S(2)}) %all-to-all-start.1) | async-done | bytes 65568 | tf_op jit(solution)/shard_map/all_to_all | solution.py:28
  (150 shorter events, 25.4 us)
Async XLA Ops:
  0.6 94.0 %copy-start = (f32[34,34]{1,0:T(8,128)S(1)}, f32[34,34]{1,0:T(8,128)}, u32[]{:S(2)}) copy-start(f32[34,34]{1,0:T(8,128)} %param.19) | copy-start | bytes 13876
  2.0 92.5 %all-to-all-start = ((f32[8,4,1024]{2,1,0:T(4,128)}), f32[8,4,1024]{2,1,0:T(4,128)S(1)}, u32[]{:S(2)}, u32[]{:S(2)}) async-start(f32[8,4,1024]{2,1,0:T(4,128)} %broadcast_in_dim.44), calls=%async_computation | async-start | bytes 262144 | tf_op jit(solution)/shard_map/all_to_all | solution.py:28
  93.4 1.0 copy-start.2
  93.8 1.2 copy-start.3
  212.9 0.6 copy-start.1
  267.1 35.6 %all-to-all-start.1 = ((f32[8,2,1024]{2,1,0:T(2,128)}), f32[8,2,1024]{2,1,0:T(2,128)S(1)}, u32[]{:S(2)}, u32[]{:S(2)}) async-start(f32[8,2,1024]{2,1,0:T(2,128)} %broadcast_in_dim.49), calls=%async_computation.1 | async-start | bytes 131072 | tf_op jit(solution)/shard_map/all_to_all | solution.py:28
where the time goes:
time: 304 us
  blocking collectives  206 us (68%)
  starting transfers between devices  40.8 us (13%)
  matrix products  36.9 us (12%)
  local copies, waits for them, and re-layouts  7.68 us (3%)
  other arithmetic  6.67 us (2%)
  waiting for transfers between devices  4.13 us (1%)
    psum x4, blocking collectives, by_axis(): return functools.reduce(lax.psum, axes, x)  98.4 us
    all_gather x1, blocking collectives, rows_first(): lax.all_gather(both, axis, axis=0, tiled=True)  77.8 us
    all_to_all x2, starting transfers between devices, sent_to_all(): return lax.all_to_all(copies, axis, split_axis=0, concat_axis=0, tiled=True)  40.8 us
    all_gather x2, blocking collectives, collected_together(): both, at, found = (lax.all_gather(jnp.concatenate(lines), axis), 0, {})  29.8 us
    dot_general x12, matrix products, contract_rank(): lax.dot_general(left_block, weighted, (((0,), (0,)), ((), ())), precision...  24.7 us
    dot_general x8, matrix products, contract_last(): lax.dot_general(former, latter, (((1,), (1,)), ((), ())), precision=HIGHE...  11.6 us
  transfers between devices with their start and end apart: 2, of which 1 were waited for; matrix products, arithmetic and copies ran while one was open for 2% of the time, Pallas kernels for 0%

commit v1 on v0

--- a/solution.py
+++ b/solution.py
@@ -15,7 +15,16 @@
 def rows_first(arrays, axis, dims):
     turned = [jnp.moveaxis(a, dim, 0) for a, dim in zip(arrays, dims)]
     both = jnp.concatenate([t.reshape(len(t), -1) for t in turned], axis=1)
-    filled, at, gathered = (lax.all_gather(both, axis, axis=0, tiled=True), 0, [])
+    filled, at, gathered = (
+        jnp.concatenate(
+            lax.all_to_all(
+                jnp.stack(lax.axis_size(axis) * [both], axis=0), axis, split_axis=0, concat_axis=0
+            ),
+            0,
+        ),
+        0,
+        [],
+    )
     for t, dim in zip(turned, dims):
         slab = filled[:, at : at + t[0].size].reshape(-1, *t.shape[1:])
         gathered.append(jnp.moveaxis(slab, 0, dim))

time: 304 us -> 243 us (0.80)
  blocking collectives: 206 us -> 104 us
  waiting for transfers between devices: 4.13 us -> 25.9 us
  starting transfers between devices: 40.8 us -> 55.1 us
    all_gather x1 -> x0, blocking collectives: 77.8 us -> none  [rows_first(): lax.all_gather(both, axis, axis=0, tiled=True)]
    psum x4, blocking collectives: 98.4 us -> 74.8 us  [by_axis(): return functools.reduce(lax.psum, axes, x)]
    all_to_all x0 -> x1, waiting for transfers between devices: none -> 19.4 us  [rows_first(): lax.all_to_all(jnp.stack(lax.axis_size(axis) * [both], axis=0), axis, spl...]
    all_to_all x0 -> x1, starting transfers between devices: none -> 14.1 us  [rows_first(): lax.all_to_all(jnp.stack(lax.axis_size(axis) * [both], axis=0), axis, spl...]
  transfers between devices with their start and end apart: 2 -> 3, of which waited for: 1 -> 3; matrix products, arithmetic and copies ran while one was open for 2% -> 2% of each run, Pallas kernels for 0% -> 0%
where the time goes in v1:
time: 243 us; the launch traced here: 242 us
  blocking collectives  104 us (43%)
  starting transfers between devices  55.1 us (23%)
  matrix products  37 us (15%)
  waiting for transfers between devices  25.9 us (11%)
  local copies, waits for them, and re-layouts  10.7 us (4%)
  other arithmetic  7.56 us (3%)
    psum x4, blocking collectives, by_axis(): return functools.reduce(lax.psum, axes, x)  74.8 us
    all_to_all x2, starting transfers between devices, sent_to_all(): return lax.all_to_all(copies, axis, split_axis=0, concat_axis=0, tiled=True)  41 us
    all_gather x2, blocking collectives, collected_together(): both, at, found = (lax.all_gather(jnp.concatenate(lines), axis), 0, {})  29.4 us
    dot_general x12, matrix products, contract_rank(): lax.dot_general(left_block, weighted, (((0,), (0,)), ((), ())), precision...  24.7 us
    all_to_all x1, waiting for transfers between devices, rows_first(): lax.all_to_all(jnp.stack(lax.axis_size(axis) * [both], axis=0), axis, spl...  19.4 us
    all_to_all x1, starting transfers between devices, rows_first(): lax.all_to_all(jnp.stack(lax.axis_size(axis) * [both], axis=0), axis, spl...  14.1 us
    dot_general x8, matrix products, contract_last(): lax.dot_general(former, latter, (((1,), (1,)), ((), ())), precision=HIGHE...  11.6 us
    all_to_all x2, waiting for transfers between devices, sent_to_all(): return lax.all_to_all(copies, axis, split_axis=0, concat_axis=0, tiled=True)  6.47 us
  transfers between devices with their start and end apart: 3, of which 3 were waited for; matrix products, arithmetic and copies ran while one was open for 2% of the time, Pallas kernels for 0%

profile of v1, /device:TPU:1, one launch (start us, length us, event | category | flops | bytes accessed | tf_op | source)
XLA Modules:
  0.0 242.0 jit_solution(16196104918787123338)
XLA Ops:
  2.1 10.1 %all-to-all-start.1 = ((f32[8,4,1024]{2,1,0:T(4,128)}), f32[8,4,1024]{2,1,0:T(4,128)S(1)}, u32[]{:S(2)}, u32[]{:S(2)}) async-start(f32[8,4,1024]{2,1,0:T(4,128)} %broadcast_in_dim.44), calls=%async_computation.1 | async-start | bytes 262144 | tf_op jit(solution)/shard_map/all_to_all | solution.py:37
  15.1 2.3 all-to-all-done.1
  17.4 14.1 %all-to-all-start = ((f32[64,1,1088]{2,1,0:T(1,128)}), f32[64,1,1088]{2,1,0:T(1,128)S(1)}, u32[]{:S(2)}, u32[]{:S(2)}) async-start(f32[64,1,1088]{2,1,0:T(1,128)} %reshape.553), calls=%async_computation | async-start | bytes 589824 | tf_op jit(solution)/shard_map/all_to_all | solution.py:20
  32.1 19.4 %all-to-all-done = f32[64,1,1088]{2,1,0:T(1,128)S(1)} async-done(((f32[64,1,1088]{2,1,0:T(1,128)}), f32[64,1,1088]{2,1,0:T(1,128)S(1)}, u32[]{:S(2)}, u32[]{:S(2)}) %all-to-all-start) | async-done | bytes 278560 | tf_op jit(solution)/shard_map/all_to_all | solution.py:20
  57.0 19.6 %while.37 = (s32[]{:T(128)}, f32[34,34]{1,0:T(8,128)S(1)}, f32[4,34,512]{2,0,1:T(4,128)S(1)}, f32[4,512]{1,0:T(4,128)S(1)}, f32[1024]{0:T(1024)S(1)}, /*index=5*...) while((s32[]{:T(128)}, f32[34,34]{1,0:T(8,128)S(1)}, ...), condition=%wide.region_3.4_spmd.clone, body=%wide.region_2.3_spmd.clone.sunk | while | flops 438069504 | bytes 4957355 | solution.py:195
  58.9 2.7 %fusion.110 = f32[512,34]{0,1:T(8,128)S(1)} fusion(f32[34,1024]{1,0:T(8,128)S(1)} %get-tuple-element.595, f32[512,1024]{1,0:T(8,128)S(1)} %fusion.109, f32[1024]{0:T(1024)S(1)} %get-tuple-element.592, f32[512]{0:T(512)S(1)} %bitcast.241, f32[1024]{0:T(1024)S(1)} %get-tuple-element.590, f32[512]{0:T(512)S(1)} %bitcast.242), kind=kOutput, calls=%fused_computation.5.clone.1 | convolution fusion | flops 217055232 | bytes 2318336 | tf_op jit(solution)/shard_map/while/body/eval_jaxpr/dot_general | solution.py:131
  63.8 2.7 %fusion.110 = f32[512,34]{0,1:T(8,128)S(1)} fusion(f32[34,1024]{1,0:T(8,128)S(1)} %get-tuple-element.595, f32[512,1024]{1,0:T(8,128)S(1)} %fusion.109, f32[1024]{0:T(1024)S(1)} %get-tuple-element.592, f32[512]{0:T(512)S(1)} %bitcast.241, f32[1024]{0:T(1024)S(1)} %get-tuple-element.590, f32[512]{0:T(512)S(1)} %bitcast.242), kind=kOutput, calls=%fused_computation.5.clone.1 | convolution fusion | flops 217055232 | bytes 2318336 | tf_op jit(solution)/shard_map/while/body/eval_jaxpr/dot_general | solution.py:131
  68.7 2.7 %fusion.110 = f32[512,34]{0,1:T(8,128)S(1)} fusion(f32[34,1024]{1,0:T(8,128)S(1)} %get-tuple-element.595, f32[512,1024]{1,0:T(8,128)S(1)} %fusion.109, f32[1024]{0:T(1024)S(1)} %get-tuple-element.592, f32[512]{0:T(512)S(1)} %bitcast.241, f32[1024]{0:T(1024)S(1)} %get-tuple-element.590, f32[512]{0:T(512)S(1)} %bitcast.242), kind=kOutput, calls=%fused_computation.5.clone.1 | convolution fusion | flops 217055232 | bytes 2318336 | tf_op jit(solution)/shard_map/while/body/eval_jaxpr/dot_general | solution.py:131
  73.6 2.7 %fusion.110 = f32[512,34]{0,1:T(8,128)S(1)} fusion(f32[34,1024]{1,0:T(8,128)S(1)} %get-tuple-element.595, f32[512,1024]{1,0:T(8,128)S(1)} %fusion.109, f32[1024]{0:T(1024)S(1)} %get-tuple-element.592, f32[512]{0:T(512)S(1)} %bitcast.241, f32[1024]{0:T(1024)S(1)} %get-tuple-element.590, f32[512]{0:T(512)S(1)} %bitcast.242), kind=kOutput, calls=%fused_computation.5.clone.1 | convolution fusion | flops 217055232 | bytes 2318336 | tf_op jit(solution)/shard_map/while/body/eval_jaxpr/dot_general | solution.py:131
  76.6 11.8 %psum.28 = f32[34,34]{1,0:T(8,128)S(1)} all-reduce(f32[34,34]{1,0:T(8,128)S(1)} %get-tuple-element.131), channel_id=1, replica_groups=mesh['src_0'=4,'src_1'=2,'tgt_0'=4,'tgt_1'=16] {'src_0'}, use_global_device_ids=true, to_apply=%region_4.5 | all-reduce | flops 1156 | bytes 9248 | tf_op jit(solution)/shard_map/psum | solution.py:52
  88.5 10.1 %psum.29 = f32[34,34]{1,0:T(8,128)S(1)} all-reduce(f32[34,34]{1,0:T(8,128)S(1)} %psum.28), channel_id=1, replica_groups=mesh['src_0'=4,'src_1'=2,'tgt_0'=4,'tgt_1'=16] {'src_1'}, use_global_device_ids=true, to_apply=%region_5.6 | all-reduce | flops 1156 | bytes 9248 | tf_op jit(solution)/shard_map/psum | solution.py:52
  98.5 13.3 %psum.30 = f32[34,34]{1,0:T(8,128)S(1)} all-reduce(f32[34,34]{1,0:T(8,128)S(1)} %psum.29), channel_id=1, replica_groups=mesh['src_0'=4,'src_1'=2,'tgt_0'=4,'tgt_1'=16] {'tgt_0'}, use_global_device_ids=true, to_apply=%region_6.7 | all-reduce | flops 1156 | bytes 9248 | tf_op jit(solution)/shard_map/psum | solution.py:52
  111.8 39.6 %psum.31 = f32[34,34]{1,0:T(8,128)S(1)} all-reduce(f32[34,34]{1,0:T(8,128)S(1)} %psum.30), channel_id=1, replica_groups=mesh['src_0'=4,'src_1'=2,'tgt_0'=4,'tgt_1'=16] {'tgt_1'}, use_global_device_ids=true, to_apply=%region_7.8 | all-reduce | flops 1156 | bytes 9248 | tf_op jit(solution)/shard_map/psum | solution.py:52
  152.0 11.3 %while.36 = (s32[]{:T(128)}, f32[4,512]{1,0:T(4,128)S(1)}, f32[4,512]{1,0:T(4,128)S(1)}, f32[1024]{0:T(1024)S(1)}, f32[1024]{0:T(1024)S(1)}, /*index=5*/f32[4,34...) while((s32[]{:T(128)}, f32[4,512]{1,0:T(4,128)S(1)}, f32[4,512]{1,0:T(4,128)S(1)}, ...), condition=%wide.region_11.12_spmd, body=%wide.region_8.11_spmd.sunk | while | flops 217578496 | bytes 4462697 | solution.py:211
  152.0 2.2 fusion.103
  154.9 2.2 fusion.103
  157.7 2.2 fusion.103
  160.5 2.2 fusion.103
  163.4 9.0 %all-gather.2 = f32[4,2,2048]{2,1,0:T(2,128)S(1)} all-gather(f32[1,2,2048]{2,1,0:T(2,128)S(1)} %maximum_bitcast_fusion.2), channel_id=2, replica_groups=mesh['src_0'=4,'src_1'=2,'tgt_0'=4,'tgt_1'=16] {'tgt_0'}, dimensions={0}, use_global_device_ids=true | all-gather | bytes 81920 | tf_op jit(solution)/shard_map/all_gather | solution.py:63
  172.5 20.4 %all-gather.3 = f32[16,2,2048]{2,1,0:T(2,128)S(1)} all-gather(f32[1,2,2048]{2,1,0:T(2,128)S(1)} %maximum_bitcast_fusion.3), channel_id=3, replica_groups=mesh['src_0'=4,'src_1'=2,'tgt_0'=4,'tgt_1'=16] {'tgt_1'}, dimensions={0}, use_global_device_ids=true | all-gather | bytes 278528 | tf_op jit(solution)/shard_map/all_gather | solution.py:63
  194.4 10.2 %while.38 = (s32[]{:T(128)}, f32[1024]{0:T(1024)S(1)}, f32[1024]{0:T(1024)S(1)}, f32[4,512]{1,0:T(4,128)S(1)}, f32[4,512]{1,0:T(4,128)S(1)}, /*index=5*/f32[4,34...) while((s32[]{:T(128)}, f32[1024]{0:T(1024)S(1)}, f32[1024]{0:T(1024)S(1)}, ...), condition=%wide.region_15.16_spmd.clone, body=%wide.region_12.15_spmd.clone.sunk | while | flops 217584640 | bytes 4505712 | solution.py:235
  194.4 2.1 fusion.112
  205.2 30.9 %all-to-all-start.2 = ((f32[8,2,1024]{2,1,0:T(2,128)}), f32[8,2,1024]{2,1,0:T(2,128)S(1)}, u32[]{:S(2)}, u32[]{:S(2)}) async-start(f32[8,2,1024]{2,1,0:T(2,128)} %broadcast_in_dim.49), calls=%async_computation.2 | async-start | bytes 131072 | tf_op jit(solution)/shard_map/all_to_all | solution.py:37
  236.9 4.1 %all-to-all-done.2 = f32[8,2,1024]{2,1,0:T(2,128)S(1)} async-done(((f32[8,2,1024]{2,1,0:T(2,128)}), f32[8,2,1024]{2,1,0:T(2,128)S(1)}, u32[]{:S(2)}, u32[]{:S(2)}) %all-to-all-start.2) | async-done | bytes 65568 | tf_op jit(solution)/shard_map/all_to_all | solution.py:37
  (156 shorter events, 33.5 us)
Async XLA Ops:
  0.6 31.2 %copy-start = (f32[34,34]{1,0:T(8,128)S(1)}, f32[34,34]{1,0:T(8,128)}, u32[]{:S(2)}) copy-start(f32[34,34]{1,0:T(8,128)} %param.19) | copy-start | bytes 13876
  0.6 31.0 %copy-start.2 = (f32[1024]{0:T(1024)S(1)}, f32[1024]{0:T(1024)}, u32[]{:S(2)}) copy-start(f32[1024]{0:T(1024)} %param.18) | copy-start | bytes 12292
  2.1 15.4 %all-to-all-start.1 = ((f32[8,4,1024]{2,1,0:T(4,128)}), f32[8,4,1024]{2,1,0:T(4,128)S(1)}, u32[]{:S(2)}, u32[]{:S(2)}) async-start(f32[8,4,1024]{2,1,0:T(4,128)} %broadcast_in_dim.44), calls=%async_computation.1 | async-start | bytes 262144 | tf_op jit(solution)/shard_map/all_to_all | solution.py:37
  17.4 34.1 %all-to-all-start = ((f32[64,1,1088]{2,1,0:T(1,128)}), f32[64,1,1088]{2,1,0:T(1,128)S(1)}, u32[]{:S(2)}, u32[]{:S(2)}) async-start(f32[64,1,1088]{2,1,0:T(1,128)} %reshape.553), calls=%async_computation | async-start | bytes 589824 | tf_op jit(solution)/shard_map/all_to_all | solution.py:20
  55.9 1.1 copy-start.3
  151.4 0.6 copy-start.1
  205.2 35.8 %all-to-all-start.2 = ((f32[8,2,1024]{2,1,0:T(2,128)}), f32[8,2,1024]{2,1,0:T(2,128)S(1)}, u32[]{:S(2)}, u32[]{:S(2)}) async-start(f32[8,2,1024]{2,1,0:T(2,128)} %broadcast_in_dim.49), calls=%async_computation.2 | async-start | bytes 131072 | tf_op jit(solution)/shard_map/all_to_all | solution.py:37
